TPU v7x, 32 devices: a whole 2x2x4 slice. The times are simulated.
32 devices in a mesh: chain: 8 (over y, x, core), col: 4 (over z).
Axes of the slice: x: 2, y: 2, z: 4, core: 2. Of those that a mesh axis runs over, the one named last changes fastest.
Arguments:
- rhs: bfloat16 [16, 64, 2560], P('chain', None, 'col'), may hold values from -6 to 6
- block_inverse: bfloat16 [16, 2560, 2560], P('chain', 'col'), as said below
- entry_factor: bfloat16 [16, 2560, 128], P('chain', 'col'), as said below
- exit_factor: bfloat16 [16, 2560, 128], P('chain', 'col'), as said below
- previous: bfloat16 [64, 2560], P(None, 'col'), may hold values from -6 to 6
Outputs:
- solution: float32 [16, 64, 2560], P('chain', None, 'col')
Inputs may be any that keep to these rules, and one draw needn't show every extreme that they name: Every block of block_inverse equals its own transpose. `entry_factor`: entries are independent, of mean zero. `exit_factor`: entries are independent, of mean zero.
All inputs are finite; a program needn't handle non-finite values.
Results may differ from a plain program's by a relative error of at most 0.0003.
Values may be sent and summed in bfloat16 or wider, within the bound.
A program may use at most 64 MiB of HBM per device.

v0:
```python
import jax
import jax.numpy as jnp
from jax import lax
from jax.sharding import PartitionSpec as P


def from_behind(block, axis, distance):
    devices = range(lax.axis_size(axis))
    route = [(i - distance, i) for i in devices if i - distance in devices]
    return lax.ppermute(block, axis, route)


def entering(part, axis, combine, identity, reverse):
    count = lax.axis_size(axis)
    place = lax.axis_index(axis)
    ahead = count - 1 - place if reverse else place
    gathered = jax.tree.map(lambda a: lax.all_gather(a, axis), part)
    state = jax.tree.map(lambda a, e: jnp.zeros_like(a) + jnp.asarray(e, a.dtype), part, identity)

    def one(step, state):
        source = count - 1 - step if reverse else step
        return combine(
            state, jax.tree.map(lambda a: lax.dynamic_index_in_dim(a, source, 0, False), gathered)
        )

    return lax.fori_loop(0, ahead, one, state)


def compose(earlier, later):
    exact = lax.Precision.HIGHEST
    first_map, first_shift = earlier
    second_map, second_shift = later
    return (
        jnp.dot(first_map, second_map, precision=exact),
        jnp.dot(first_shift, second_map, precision=exact) + second_shift,
    )


def shards(rhs, block_inverse, entry_factor, exit_factor, previous):
    exact = lax.Precision.HIGHEST
    intervals_here = rhs.shape[0]
    column_count = rhs.shape[1]
    state_width = entry_factor.shape[2]
    arriving = from_behind(exit_factor[:1], "chain", -1)
    following = jnp.concatenate([exit_factor[1:], arriving], axis=0)
    couple_part = -jnp.einsum(
        "irn,irm->inm", entry_factor, following, preferred_element_type=jnp.float32
    )
    source_part = jnp.einsum("icr,irm->icm", rhs, following, preferred_element_type=jnp.float32)
    opening_part = jnp.dot(previous, exit_factor[0], preferred_element_type=jnp.float32)
    couple, source, opening = lax.psum((couple_part, source_part, opening_part), "col")
    identity = jnp.eye(state_width, dtype=jnp.float32)
    empty_shift = jnp.zeros((column_count, state_width), jnp.float32)
    first_chain = lax.axis_index("chain") == 0
    matrix = identity
    offset = empty_shift
    for position in range(intervals_here):
        matrix = jnp.dot(matrix, couple[position], precision=exact)
        offset = jnp.dot(offset, couple[position], precision=exact) + source[position]
    folded = jnp.dot(opening, matrix, precision=exact) + offset
    offset = jnp.where(first_chain, folded, offset)
    matrix = jnp.where(first_chain, jnp.zeros_like(matrix), matrix)
    _, incoming = entering((matrix, offset), "chain", compose, (identity, empty_shift), False)
    carry_state = jnp.where(first_chain, opening, incoming)
    solved_list = []
    for position in range(intervals_here):
        solved_list.append(
            rhs[position].astype(jnp.float32)
            - jnp.dot(carry_state, entry_factor[position].astype(jnp.float32).T, precision=exact)
        )
        carry_state = jnp.dot(carry_state, couple[position], precision=exact) + source[position]
    forward = jnp.stack(solved_list).astype(jnp.bfloat16)
    applied = jnp.einsum(
        "icb,irb->icr",
        lax.all_gather(forward, "col", axis=2, tiled=True),
        block_inverse,
        preferred_element_type=jnp.float32,
    )
    carried_part = jnp.einsum(
        "icr,irn->icn",
        applied.astype(jnp.bfloat16),
        entry_factor,
        preferred_element_type=jnp.float32,
    )
    carried = lax.psum(carried_part, "col")
    last_chain = lax.axis_index("chain") == lax.axis_size("chain") - 1
    matrix = identity
    offset = empty_shift
    for position in reversed(range(intervals_here)):
        turned = couple[position].T
        matrix = jnp.dot(matrix, turned, precision=exact)
        offset = jnp.dot(offset, turned, precision=exact) + carried[position]
    matrix = jnp.where(last_chain, jnp.zeros_like(matrix), matrix)
    _, behind = entering((matrix, offset), "chain", compose, (identity, empty_shift), True)
    results = [None] * intervals_here
    for position in reversed(range(intervals_here)):
        results[position] = applied[position] - jnp.dot(
            behind, following[position].astype(jnp.float32).T, precision=exact
        )
        behind = jnp.dot(behind, couple[position].T, precision=exact) + carried[position]
    return jnp.stack(results)


def solution(mesh):
    placed = (
        P("chain", None, "col"),
        P("chain", "col", None),
        P("chain", "col", None),
        P("chain", "col", None),
        P(None, "col"),
    )
    return jax.shard_map(
        shards, mesh=mesh, in_specs=placed, out_specs=P("chain", None, "col"), check_vma=False
    )
```

profile of v0, /device:TPU:0, one launch (start us, length us, event | category | flops | bytes accessed | tf_op | source)
XLA Modules:
  0.0 161.5 jit_solution(1179635024437629665)
XLA Ops:
  6.5 1.1 fusion.37
  7.8 1.3 collective-permute-start
  9.3 1.8 %collective-permute-done = bf16[1,640,128]{1,2,0:T(8,128)(2,1)S(1)} collective-permute-done((bf16[1,640,128]{1,2,0:T(8,128)(2,1)S(1)}, bf16[1,640,128]{1,2,0:T(8,128)(2,1)S(1)}, u32[]{:S(2)}, u32[]{:S(2)}) %collective-permute-start) | collective-permute-done | bytes 163872 | tf_op jit(solution)/shard_map/ppermute | solution.py:10
  11.1 1.8 %convolution_bitcast_fusion.2 = f32[2,64,128]{2,1,0:T(8,128)} fusion(bf16[2,64,640]{2,1,0:T(8,128)(2,1)} %param.9, bf16[1,640,128]{1,2,0:T(8,128)(2,1)S(1)} %collective-permute-done, bf16[1,640,128]{1,2,0:T(8,128)(2,1)S(1)} %copy.11), kind=kOutput, calls=%fused_computation.23 | convolution fusion | flops 21135360 | bytes 557056 | tf_op jit(solution)/shard_map/icr,irm->icm/dot_general | solution.py:49
  12.9 1.9 %fusion.10 = f32[2,128,128]{1,2,0:T(8,128)} fusion(bf16[2,640,128]{2,1,0:T(8,128)(2,1)} %param.11, bf16[1,640,128]{1,2,0:T(8,128)(2,1)S(1)} %collective-permute-done, bf16[1,640,128]{1,2,0:T(8,128)(2,1)S(1)} %copy.11), kind=kOutput, calls=%fused_computation.17 | convolution fusion | flops 42139648 | bytes 786432 | tf_op jit(solution)/shard_map/irn,irm->inm/dot_general | solution.py:46
  14.8 1.1 fusion.17
  15.9 21.0 %psum.28 = f32[64,128]{1,0:T(8,128)S(1)} all-reduce(f32[64,128]{1,0:T(8,128)S(1)} %fusion.17), channel_id=1, replica_groups=mesh['chain'=8,'col'=4] {'col'}, use_global_device_ids=true, to_apply=%region_0.0 | all-reduce | flops 8192 | bytes 65536 | tf_op jit(solution)/shard_map/psum | solution.py:51
  36.9 18.5 %all-reduce.6.cloned.1.call-done = (f32[2,128,128]{1,2,0:T(8,128)}, f32[2,64,128]{2,1,0:T(8,128)}) async-done(((f32[2,128,128]{1,2,0:T(8,128)}, f32[2,64,128]{2,1,0:T(8,128)}), (f32[2,128,128]{1,2,0:T(8,128)}, f32[2,64,128]{2,1,0:T(8,128)})) %all-reduce.6.cloned.1.call-update) | async-done | bytes 196624 | tf_op jit(solution)/shard_map/psum | solution.py:51
  55.4 1.1 fusion.27
  56.5 1.1 convolution_add_fusion.5
  57.6 1.1 convolution_add_fusion.4
  58.7 1.1 broadcast_select_fusion
  60.0 9.2 %all-gather.1 = f32[512,128]{1,0:T(8,128)S(1)} all-gather(f32[64,128]{1,0:T(8,128)S(1)} %fusion.15), channel_id=3, replica_groups=mesh['chain'=8,'col'=4] {'chain'}, dimensions={0}, use_global_device_ids=true | all-gather | bytes 294912 | tf_op jit(solution)/shard_map/all_gather | solution.py:17
  69.2 9.8 %all-gather = f32[1024,128]{1,0:T(8,128)S(1)} all-gather(f32[128,128]{1,0:T(8,128)S(1)} %get-tuple-element.159), channel_id=2, replica_groups=mesh['chain'=8,'col'=4] {'chain'}, dimensions={0}, use_global_device_ids=true | all-gather | bytes 589824 | tf_op jit(solution)/shard_map/all_gather | solution.py:17
  79.0 0.3 fusion.14
  79.3 1.1 convolution_add_fusion.3
  80.5 1.0 fusion.26
  81.5 0.3 fusion.13
  81.9 17.2 %all_gather.31 = bf16[2,64,2560]{2,1,0:T(8,128)(2,1)S(1)} all-gather(bf16[2,64,640]{2,1,0:T(8,128)(2,1)S(1)} %pad_maximum_fusion.4), channel_id=1, replica_groups=mesh['chain'=8,'col'=4] {'col'}, dimensions={2}, use_global_device_ids=true | all-gather | bytes 819200 | tf_op jit(solution)/shard_map/all_gather | solution.py:75
  99.1 4.9 %fusion.38 = f32[2,64,640]{2,1,0:T(8,128)S(1)} fusion(bf16[2,64,2560]{2,1,0:T(8,128)(2,1)S(1)} %all_gather.31, bf16[2,640,2560]{2,1,0:T(8,128)(2,1)} %param.10), kind=kOutput, calls=%fused_computation.68 | convolution fusion | flops 419430400 | bytes 7536640 | tf_op jit(solution)/shard_map/icb,irb->icr/dot_general | solution.py:73
  104.0 0.8 fusion.22
  104.9 0.2 convolution_select_fusion
  105.1 9.9 %all-gather.2 = f32[1024,128]{1,0:T(8,128)S(1)} all-gather(f32[128,128]{1,0:T(8,128)S(1)} %convolution_select_fusion), channel_id=4, replica_groups=mesh['chain'=8,'col'=4] {'chain'}, dimensions={0}, use_global_device_ids=true | all-gather | bytes 589824 | tf_op jit(solution)/shard_map/all_gather | solution.py:17
  115.0 24.6 %all-reduce.4.cloned.1.call-done = f32[2,64,128]{2,1,0:T(8,128)} async-done(((f32[2,64,128]{2,1,0:T(8,128)}), f32[2,64,128]{2,1,0:T(8,128)}) %all-reduce.4.cloned.1.call-update) | async-done | bytes 65552 | tf_op jit(solution)/shard_map/psum | solution.py:85
  139.6 0.9 convolution_add_fusion.2
  140.5 0.9 convolution_add_fusion.1
  141.5 9.3 %all-gather.3 = f32[512,128]{1,0:T(8,128)S(1)} all-gather(f32[64,128]{1,0:T(8,128)S(1)} %convolution_add_fusion.1), channel_id=5, replica_groups=mesh['chain'=8,'col'=4] {'chain'}, dimensions={0}, use_global_device_ids=true | all-gather | bytes 294912 | tf_op jit(solution)/shard_map/all_gather | solution.py:17
  150.8 1.6 %while.27 = (s32[]{:T(128)}, f32[64,128]{1,0:T(8,128)S(1)}, s32[]{:T(128)}, f32[8,128,128]{2,1,0:T(8,128)S(1)}, f32[8,64,128]{2,1,0:T(8,128)S(1)}, /*index=5*/s32[]{:T(128)}, s32[]{:T(128)}, s32[]{:T(128)}, s32[]{:T(128)}) while((s32[]{:T(128)}, f32[64,128]{1,0:T(8,128)S(1)}, s32[]{:T(128)}, f32[8,128,128]{2,1,0:T(8,128)S(1)}, ...), condition=%wide.region_7.8_spmd, body=%wide.region_6.7_spmd.sunk | while | flops 12591110 | bytes 230539 | solution.py:26
  152.4 0.9 convolution_add_fusion
  153.4 0.3 fusion.9
  153.7 0.2 fusion.8
  153.9 0.7 pad_maximum_fusion.1
  (35 shorter events, 2.0 us)
Async XLA Ops:
  6.5 8.3 %copy-start = (bf16[64,640]{1,0:T(8,128)(2,1)S(1)}, bf16[64,640]{1,0:T(8,128)(2,1)}, u32[]{:S(2)}) copy-start(bf16[64,640]{1,0:T(8,128)(2,1)} %param.13) | copy-start | bytes 245764
  6.5 72.5 %copy-start.4 = (bf16[2,64,640]{2,1,0:T(8,128)(2,1)S(1)}, bf16[2,64,640]{2,1,0:T(8,128)(2,1)}, u32[]{:S(2)}) copy-start(bf16[2,64,640]{2,1,0:T(8,128)(2,1)} %param.9) | copy-start | bytes 491524
  6.5 72.5 %copy-start.2 = (bf16[2,640,128]{2,1,0:T(8,128)(2,1)S(1)}, bf16[2,640,128]{2,1,0:T(8,128)(2,1)}, u32[]{:S(2)}) copy-start(bf16[2,640,128]{2,1,0:T(8,128)(2,1)} %param.11) | copy-start | bytes 983044
  6.5 48.9 %all-reduce.6.cloned.1.call-start = ((), (), s32[]{:S(2)}) async-start(), calls=%async_computation.1 | async-start | bytes 393216 | tf_op jit(solution)/shard_map/psum | solution.py:51
  7.8 3.3 %collective-permute-start = (bf16[1,640,128]{1,2,0:T(8,128)(2,1)S(1)}, bf16[1,640,128]{1,2,0:T(8,128)(2,1)S(1)}, u32[]{:S(2)}, u32[]{:S(2)}) collective-permute-start(bf16[1,640,128]{1,2,0:T(8,128)(2,1)S(1)} %copy.10), channel_id=1, source_target_pairs={{4,0},{8,4},{12,8},{16,12},{20,16},{24,20},{28,24},{5,1},{9,5},{13... | collective-permute-start | bytes 491528 | tf_op jit(solution)/shard_map/ppermute | solution.py:10
  14.8 124.8 %all-reduce.4.cloned.1.call-start = ((), (), s32[]{:S(2)}) async-start(), calls=%async_computation | async-start | bytes 131072 | tf_op jit(solution)/shard_map/psum | solution.py:85
  59.8 45.1 %copy-start.1 = (f32[2,128,128]{1,2,0:T(8,128)S(1)}, f32[2,128,128]{1,2,0:T(8,128)}, u32[]{:S(2)}) copy-start(f32[2,128,128]{1,2,0:T(8,128)} %get-tuple-element.155) | copy-start | bytes 393220
  79.3 74.0 %copy-start.3 = (bf16[2,640,128]{2,1,0:T(8,128)(2,1)S(1)}, bf16[2,640,128]{2,1,0:T(8,128)(2,1)}, u32[]{:S(2)}) copy-start(bf16[2,640,128]{2,1,0:T(8,128)(2,1)} %param.12) | copy-start | bytes 983044
Sparse Core Ops, SparseCore 0:
  14.9 40.4 all-reduce.5
  105.0 34.5 all-reduce.3
where the time goes:
time: 162 us; the launch traced here: 161 us
  blocking collectives  76.4 us (47%)
  waiting for transfers between devices  45 us (28%)
  matrix products  22.7 us (14%)
  between operations  13.6 us (8%)
    all_gather x4, blocking collectives, entering(): gathered = jax.tree.map(lambda a: lax.all_gather(a, axis), part)  38.2 us
    psum x1, waiting for transfers between devices, shards(): carried = lax.psum(carried_part, 'col')  24.6 us
    psum x1, blocking collectives, shards(): lax.psum((couple_part, source_part, opening_part), 'col')  21 us
    psum x1, waiting for transfers between devices, shards(): lax.psum((couple_part, source_part, opening_part), 'col')  18.5 us
    all_gather x1, blocking collectives, shards(): lax.all_gather(forward, 'col', axis=2, tiled=True)  17.2 us
    dot_general x1, matrix products, shards(): jnp.einsum('icb,irb->icr', lax.all_gather(forward, 'col', axis=2, tiled=T...  4.94 us
  transfers between devices with their start and end apart: 3, of which 3 were waited for; matrix products, arithmetic and copies ran while one was open for 1% of the time, Pallas kernels for 0%

commit v1 on v0

--- a/solution.py
+++ b/solution.py
@@ -82,7 +82,7 @@
         entry_factor,
         preferred_element_type=jnp.float32,
     )
-    carried = lax.psum(carried_part, "col")
+    carried = jnp.sum(jax.lax.all_gather(carried_part, "col"), axis=0)
     last_chain = lax.axis_index("chain") == lax.axis_size("chain") - 1
     matrix = identity
     offset = empty_shift

time: 162 us -> 149 us (0.920)
  waiting for transfers between devices: 45 us -> 20.5 us
  blocking collectives: 76.4 us -> 91.1 us
  matrix products: 22.7 us -> 19.8 us
    psum x1 -> x0, waiting for transfers between devices: 24.6 us -> none  [shards(): carried = lax.psum(carried_part, 'col')]
    all_gather x0 -> x1, blocking collectives: none -> 14.1 us  [shards(): carried = jnp.sum(jax.lax.all_gather(carried_part, 'col'), axis=0)]
  transfers between devices with their start and end apart: 3 -> 2, of which waited for: 3 -> 2; matrix products, arithmetic and copies ran while one was open for 1% -> 1% of each run, Pallas kernels for 0% -> 0%
where the time goes in v1:
time: 149 us
  blocking collectives  91.1 us (61%)
  waiting for transfers between devices  20.5 us (14%)
  matrix products  19.8 us (13%)
  between operations  13.6 us (9%)
    all_gather x4, blocking collectives, entering(): gathered = jax.tree.map(lambda a: lax.all_gather(a, axis), part)  38.7 us
    psum x1, blocking collectives, shards(): lax.psum((couple_part, source_part, opening_part), 'col')  20.9 us
    psum x1, waiting for transfers between devices, shards(): lax.psum((couple_part, source_part, opening_part), 'col')  18.7 us
    all_gather x1, blocking collectives, shards(): lax.all_gather(forward, 'col', axis=2, tiled=True)  17.3 us
    all_gather x1, blocking collectives, shards(): carried = jnp.sum(jax.lax.all_gather(carried_part, 'col'), axis=0)  14.1 us
    dot_general x1, matrix products, shards(): jnp.einsum('icb,irb->icr', lax.all_gather(forward, 'col', axis=2, tiled=T...  4.94 us
  transfers between devices with their start and end apart: 2, of which 2 were waited for; matrix products, arithmetic and copies ran while one was open for 1% of the time, Pallas kernels for 0%

profile of v1, /device:TPU:0, one launch (start us, length us, event | category | flops | bytes accessed | tf_op | source)
XLA Modules:
  0.0 148.7 jit_solution(4744948512112829492)
XLA Ops:
  6.5 1.1 fusion.37
  7.8 1.3 collective-permute-start
  9.3 1.8 %collective-permute-done = bf16[1,640,128]{1,2,0:T(8,128)(2,1)S(1)} collective-permute-done((bf16[1,640,128]{1,2,0:T(8,128)(2,1)S(1)}, bf16[1,640,128]{1,2,0:T(8,128)(2,1)S(1)}, u32[]{:S(2)}, u32[]{:S(2)}) %collective-permute-start) | collective-permute-done | bytes 163872 | tf_op jit(solution)/shard_map/ppermute | solution.py:10
  11.1 1.8 %convolution_bitcast_fusion.2 = f32[2,64,128]{2,1,0:T(8,128)} fusion(bf16[2,64,640]{2,1,0:T(8,128)(2,1)} %param.9, bf16[1,640,128]{1,2,0:T(8,128)(2,1)S(1)} %collective-permute-done, bf16[1,640,128]{1,2,0:T(8,128)(2,1)S(1)} %copy.14), kind=kOutput, calls=%fused_computation.23 | convolution fusion | flops 21135360 | bytes 557056 | tf_op jit(solution)/shard_map/icr,irm->icm/dot_general | solution.py:49
  12.9 1.9 %fusion.10 = f32[2,128,128]{1,2,0:T(8,128)} fusion(bf16[2,640,128]{2,1,0:T(8,128)(2,1)} %param.11, bf16[1,640,128]{1,2,0:T(8,128)(2,1)S(1)} %collective-permute-done, bf16[1,640,128]{1,2,0:T(8,128)(2,1)S(1)} %copy.14), kind=kOutput, calls=%fused_computation.17 | convolution fusion | flops 42139648 | bytes 786432 | tf_op jit(solution)/shard_map/irn,irm->inm/dot_general | solution.py:46
  14.8 1.1 fusion.17
  15.9 20.9 %psum.21 = f32[64,128]{1,0:T(8,128)S(1)} all-reduce(f32[64,128]{1,0:T(8,128)S(1)} %fusion.17), channel_id=1, replica_groups=mesh['chain'=8,'col'=4] {'col'}, use_global_device_ids=true, to_apply=%region_0.0 | all-reduce | flops 8192 | bytes 65536 | tf_op jit(solution)/shard_map/psum | solution.py:51
  36.8 18.7 %all-reduce.3.cloned.1.call-done = (f32[2,128,128]{1,2,0:T(8,128)}, f32[2,64,128]{2,1,0:T(8,128)}) async-done(((f32[2,128,128]{1,2,0:T(8,128)}, f32[2,64,128]{2,1,0:T(8,128)}), (f32[2,128,128]{1,2,0:T(8,128)}, f32[2,64,128]{2,1,0:T(8,128)})) %all-reduce.3.cloned.1.call-update) | async-done | bytes 196624 | tf_op jit(solution)/shard_map/psum | solution.py:51
  55.5 1.1 fusion.27
  56.5 1.1 convolution_add_fusion.5
  57.6 1.1 convolution_add_fusion.4
  58.7 1.1 broadcast_select_fusion
  60.0 9.2 %all-gather.1 = f32[512,128]{1,0:T(8,128)S(1)} all-gather(f32[64,128]{1,0:T(8,128)S(1)} %fusion.15), channel_id=3, replica_groups=mesh['chain'=8,'col'=4] {'chain'}, dimensions={0}, use_global_device_ids=true | all-gather | bytes 294912 | tf_op jit(solution)/shard_map/all_gather | solution.py:17
  69.2 9.9 %all-gather = f32[1024,128]{1,0:T(8,128)S(1)} all-gather(f32[128,128]{1,0:T(8,128)S(1)} %get-tuple-element.159), channel_id=2, replica_groups=mesh['chain'=8,'col'=4] {'chain'}, dimensions={0}, use_global_device_ids=true | all-gather | bytes 589824 | tf_op jit(solution)/shard_map/all_gather | solution.py:17
  79.2 0.3 fusion.14
  79.5 1.1 convolution_add_fusion.3
  80.6 1.0 fusion.26
  81.6 0.3 fusion.13
  82.0 17.3 %all_gather.37 = bf16[2,64,2560]{2,1,0:T(8,128)(2,1)S(1)} all-gather(bf16[2,64,640]{2,1,0:T(8,128)(2,1)S(1)} %pad_maximum_fusion.4), channel_id=1, replica_groups=mesh['chain'=8,'col'=4] {'col'}, dimensions={2}, use_global_device_ids=true | all-gather | bytes 819200 | tf_op jit(solution)/shard_map/all_gather | solution.py:75
  99.3 4.9 %fusion.38 = f32[2,64,640]{2,1,0:T(8,128)S(1)} fusion(bf16[2,64,2560]{2,1,0:T(8,128)(2,1)S(1)} %all_gather.37, bf16[2,640,2560]{2,1,0:T(8,128)(2,1)} %param.10), kind=kOutput, calls=%fused_computation.68 | convolution fusion | flops 419430400 | bytes 7536640 | tf_op jit(solution)/shard_map/icb,irb->icr/dot_general | solution.py:73
  104.5 14.1 %all-gather.3 = f32[8,64,128]{2,1,0:T(8,128)S(1)} all-gather(f32[2,64,128]{2,1,0:T(8,128)S(1)} %fusion.22), channel_id=5, replica_groups=mesh['chain'=8,'col'=4] {'col'}, dimensions={0}, use_global_device_ids=true | all-gather | bytes 327680 | tf_op jit(solution)/shard_map/all_gather | solution.py:85
  119.0 9.4 %all-gather.4 = f32[512,128]{1,0:T(8,128)S(1)} all-gather(f32[64,128]{1,0:T(8,128)S(1)} %convolution_add_fusion.1), channel_id=6, replica_groups=mesh['chain'=8,'col'=4] {'chain'}, dimensions={0}, use_global_device_ids=true | all-gather | bytes 294912 | tf_op jit(solution)/shard_map/all_gather | solution.py:17
  128.4 0.2 convolution_select_fusion
  128.6 10.2 %all-gather.2 = f32[1024,128]{1,0:T(8,128)S(1)} all-gather(f32[128,128]{1,0:T(8,128)S(1)} %convolution_select_fusion), channel_id=4, replica_groups=mesh['chain'=8,'col'=4] {'chain'}, dimensions={0}, use_global_device_ids=true | all-gather | bytes 589824 | tf_op jit(solution)/shard_map/all_gather | solution.py:17
  138.8 1.6 %while.27 = (s32[]{:T(128)}, f32[64,128]{1,0:T(8,128)S(1)}, s32[]{:T(128)}, f32[8,128,128]{2,1,0:T(8,128)S(1)}, f32[8,64,128]{2,1,0:T(8,128)S(1)}, /*index=5*/s32[]{:T(128)}, s32[]{:T(128)}, s32[]{:T(128)}, s32[]{:T(128)}) while((s32[]{:T(128)}, f32[64,128]{1,0:T(8,128)S(1)}, s32[]{:T(128)}, f32[8,128,128]{2,1,0:T(8,128)S(1)}, ...), condition=%wide.region_7.8_spmd, body=%wide.region_6.7_spmd.sunk | while | flops 12591110 | bytes 230539 | solution.py:26
  139.0 0.2 fusion.68
  139.2 0.2 fusion.68
  139.5 0.2 fusion.68
  139.7 0.2 fusion.68
  140.6 0.3 fusion.9
  140.9 0.2 fusion.8
  141.1 0.8 pad_maximum_fusion.1
  (34 shorter events, 1.9 us)
Async XLA Ops:
  6.5 8.2 %copy-start = (bf16[64,640]{1,0:T(8,128)(2,1)S(1)}, bf16[64,640]{1,0:T(8,128)(2,1)}, u32[]{:S(2)}) copy-start(bf16[64,640]{1,0:T(8,128)(2,1)} %param.13) | copy-start | bytes 245764
  6.5 72.6 %copy-start.4 = (bf16[2,64,640]{2,1,0:T(8,128)(2,1)S(1)}, bf16[2,64,640]{2,1,0:T(8,128)(2,1)}, u32[]{:S(2)}) copy-start(bf16[2,64,640]{2,1,0:T(8,128)(2,1)} %param.9) | copy-start | bytes 491524
  6.5 72.6 %copy-start.2 = (bf16[2,640,128]{2,1,0:T(8,128)(2,1)S(1)}, bf16[2,640,128]{2,1,0:T(8,128)(2,1)}, u32[]{:S(2)}) copy-start(bf16[2,640,128]{2,1,0:T(8,128)(2,1)} %param.11) | copy-start | bytes 983044
  6.5 48.9 %all-reduce.3.cloned.1.call-start = ((), (), s32[]{:S(2)}) async-start(), calls=%async_computation | async-start | bytes 393216 | tf_op jit(solution)/shard_map/psum | solution.py:51
  7.8 3.3 %collective-permute-start = (bf16[1,640,128]{1,2,0:T(8,128)(2,1)S(1)}, bf16[1,640,128]{1,2,0:T(8,128)(2,1)S(1)}, u32[]{:S(2)}, u32[]{:S(2)}) collective-permute-start(bf16[1,640,128]{1,2,0:T(8,128)(2,1)S(1)} %copy.13), channel_id=1, source_target_pairs={{4,0},{8,4},{12,8},{16,12},{20,16},{24,20},{28,24},{5,1},{9,5},{13... | collective-permute-start | bytes 491528 | tf_op jit(solution)/shard_map/ppermute | solution.py:10
  69.2 49.3 %copy-start.1 = (f32[2,128,128]{1,2,0:T(8,128)S(1)}, f32[2,128,128]{1,2,0:T(8,128)}, u32[]{:S(2)}) copy-start(f32[2,128,128]{1,2,0:T(8,128)} %get-tuple-element.155) | copy-start | bytes 393220
  82.0 58.6 %copy-start.3 = (bf16[2,640,128]{2,1,0:T(8,128)(2,1)S(1)}, bf16[2,640,128]{2,1,0:T(8,128)(2,1)}, u32[]{:S(2)}) copy-start(bf16[2,640,128]{2,1,0:T(8,128)(2,1)} %param.12) | copy-start | bytes 983044
Sparse Core Ops, SparseCore 0:
  14.9 40.5 all-reduce.2
